TPU v7x, 32 devices: a whole 2x2x4 slice. The times are simulated.
32 devices in a mesh: tm: 4 (over y, core), space: 8 (over z, x).
Axes of the slice: x: 2, y: 2, z: 4, core: 2. Of those that a mesh axis runs over, the one named last changes fastest.
Arguments:
- perm_field: float32 [4, 32, 32, 256], P(None, 'space'), may hold values from 0.5 to 2
- step_multiplier: float32 [4, 32, 32, 256], P('tm', 'space'), may hold values from 0.5 to 2
- inflow: float32 [4, 32, 32, 256], P('tm', 'space'), may hold values from -3 to 3
- start_pressure: float32 [32, 32, 256], P('space'), may hold values from -6 to 6
- start_saturation: float32 [32, 32, 256], P('space'), may hold values from 0.1 to 0.9
- region_ids: int32 [32, 32, 256], P('space'), may hold values from 0 to 7
- region_table: float32 [3, 8], replicated, may hold values from 0.25 to 2
- well_cells: int32 [32], replicated, may hold values from 0 to 262143
- well_rates: float32 [4, 32], P('tm'), may hold values from -8 to 8
- observed: float32 [4, 4, 32], P(None, 'tm'), may hold values from -6 to 6
Outputs:
- misfit: float32 [4], replicated
- slab_pressure: float32 [4, 4, 32, 32, 256], P('tm', None, 'space')
- slab_saturation: float32 [4, 4, 32, 32, 256], P('tm', None, 'space')
All inputs are finite; a program needn't handle non-finite values.
Results may differ from a plain program's by a relative error of at most 0.0003.
Values sent between devices are 32-bit elements; how exact they have to be, the bound alone decides.
A program may use at most 64 MiB of HBM per device.

v0:
```python
import jax
import jax.numpy as jnp
from jax import lax
from jax.sharding import PartitionSpec as P

MB = 1
REP_DEV = 1
ITERS = 3


def padded(cells, sides, width):
    for axis, dim in sides:
        count = lax.axis_size(axis)
        ends = count - 1
        head = lax.slice_in_dim(cells, 0, width, axis=dim)
        tail = lax.slice_in_dim(cells, cells.shape[dim] - width, cells.shape[dim], axis=dim)
        cells = jnp.concatenate(
            [
                lax.ppermute(tail, axis, [(i, (i + 1) % count) for i in range(ends)]),
                cells,
                lax.ppermute(head, axis, [((i + 1) % count, i) for i in range(ends)]),
            ],
            axis=dim,
        )
    return cells


def shifted(values, dimension, offset):
    margins = [(0, 0)] * values.ndim
    length = values.shape[dimension]
    if offset > 0:
        margins[dimension] = (1, 0)
        return lax.slice_in_dim(jnp.pad(values, margins), 0, length, axis=dimension)
    margins[dimension] = (0, 1)
    return lax.slice_in_dim(jnp.pad(values, margins), 1, length + 1, axis=dimension)


def neighbour_values(values_ext):
    middle = values_ext[:, 1:-1]
    return (
        values_ext[:, :-2],
        values_ext[:, 2:],
        shifted(middle, 2, 1),
        shifted(middle, 2, -1),
        shifted(middle, 3, 1),
        shifted(middle, 3, -1),
    )


def coefficients(conduct_ext):
    middle = conduct_ext[:, 1:-1]
    others = neighbour_values(conduct_ext)
    links = [jnp.sqrt(middle * other_side) for other_side in others]
    link_total = links[0] + links[1] + links[2] + links[3] + links[4] + links[5]
    return tuple(links) + (link_total,)


def jacobi_sweep(pressure_ext, couplings, storage, right_side):
    beside = neighbour_values(pressure_ext)
    inflowing = couplings[0] * beside[0]
    for link_index in range(1, 6):
        inflowing = inflowing + couplings[link_index] * beside[link_index]
    divisor = jnp.where(storage > 0, storage + couplings[6], 1.0)
    return (right_side + inflowing) / divisor


def fraction(saturation, ratio):
    squared = saturation * saturation
    remain = (1.0 - saturation) * (1.0 - saturation)
    return squared / (squared + ratio * remain)


def transport(pressure_ext, flow_ext, couplings, saturation, gain, source):
    centre_p = pressure_ext[:, 1:-1]
    centre_f = flow_ext[:, 1:-1]
    other_p = neighbour_values(pressure_ext)
    other_f = neighbour_values(flow_ext)
    outflow = None
    for link_index in range(6):
        face_flux = couplings[link_index] * (centre_p - other_p[link_index])
        carried = face_flux * jnp.where(face_flux > 0, centre_f, other_f[link_index])
        outflow = carried if outflow is None else outflow + carried
    gained = (
        jnp.maximum(source, 0.0) * (1.0 - saturation)
        - jnp.maximum(-source, 0.0) * centre_f
        - outflow
    )
    return saturation + gain * gained


def region_fields(region_ids, region_table):
    fields = []
    for table_row in range(3):
        summed = jnp.zeros(region_ids.shape, jnp.float32)
        for region_index in range(region_table.shape[1]):
            summed = summed + jnp.where(
                region_ids == region_index, region_table[table_row, region_index], 0.0
            )
        fields.append(summed)
    return (fields[0], fields[1], 0.1 * fields[2])


def advance(pressure, saturation, conduct, source, inflow_now, storage, ratio, gain):
    right_side = storage * pressure + source + inflow_now
    flow_frac = fraction(saturation, ratio)
    edges = padded(jnp.stack([conduct, pressure]), (("space", 2),), 1)
    couplings = coefficients(edges[0])
    iterate_ext = edges[1]
    iterate = pressure
    for sweep_index in range(ITERS):
        if sweep_index > 0:
            iterate_ext = padded(iterate, (("space", 1),), 1)
        iterate = jacobi_sweep(iterate_ext, couplings, storage, right_side)
    both = padded(jnp.stack([iterate, flow_frac]), (("space", 2),), 1)
    saturation = transport(both[0], both[1], couplings, saturation, gain, source)
    return (iterate, saturation)


def body(
    perm_field,
    step_multiplier,
    inflow,
    start_pressure,
    start_saturation,
    region_ids,
    region_table,
    well_cells,
    well_rates,
    observed,
):
    sections = lax.axis_size("tm")
    section_index = lax.axis_index("tm")
    space_index = lax.axis_index("space")
    grid_shape = start_pressure.shape
    width_x, depth, across = grid_shape
    batch_size = MB
    storage, ratio, gain = region_fields(region_ids, region_table)
    layer_ids = lax.broadcasted_iota(jnp.int32, grid_shape, 0) + space_index * width_x
    cell_ids = (
        layer_ids * depth + lax.broadcasted_iota(jnp.int32, grid_shape, 1)
    ) * across + lax.broadcasted_iota(jnp.int32, grid_shape, 2)
    well_picks = (well_cells[:, None] == cell_ids.reshape(1, -1)).astype(jnp.float32)
    well_owned = jnp.sum(well_picks, axis=1)
    start_p = jnp.broadcast_to(start_pressure, (batch_size,) + grid_shape)
    start_s = jnp.broadcast_to(start_saturation, (batch_size,) + grid_shape)

    def mismatch(pressure, measured):
        predicted = jnp.dot(
            pressure.reshape(batch_size, -1), well_picks.T, precision=lax.Precision.HIGHEST
        )
        return jnp.sum(well_owned * (predicted - measured) ** 2, axis=1)

    misfit = jnp.zeros((perm_field.shape[0],), jnp.float32)
    fields = (
        lax.all_gather(step_multiplier, "tm", axis=0, tiled=True),
        lax.all_gather(inflow, "tm", axis=0, tiled=True),
        lax.all_gather(well_rates, "tm", axis=0, tiled=True),
    )
    measured_all = lax.all_to_all(observed, "tm", split_axis=0, concat_axis=1, tiled=True)
    perm_rows = lax.dynamic_slice_in_dim(perm_field, section_index * batch_size, batch_size, 0)
    rate_rows = fields[2]
    placed = jnp.dot(rate_rows, well_picks, precision=lax.Precision.HIGHEST)
    all_sources = placed.reshape((rate_rows.shape[0],) + grid_shape)
    zero_ends = jnp.zeros((sections, batch_size) + grid_shape, jnp.float32)

    def one_section(slab_index, state_tuple):
        pressure, saturation, ends_p, ends_s, errors = state_tuple
        position = slab_index * REP_DEV + 0
        multiplier = lax.dynamic_index_in_dim(fields[0], position, 0, keepdims=False)
        inflow_now = lax.dynamic_index_in_dim(fields[1], position, 0, keepdims=False)
        source = lax.dynamic_index_in_dim(all_sources, position, 0, keepdims=False)
        pressure, saturation = advance(
            pressure, saturation, perm_rows * multiplier, source, inflow_now, storage, ratio, gain
        )
        errors = errors + mismatch(
            pressure, lax.dynamic_index_in_dim(measured_all, position, 1, keepdims=False)
        )
        ends_p = lax.dynamic_update_index_in_dim(ends_p, pressure, slab_index, 0)
        ends_s = lax.dynamic_update_index_in_dim(ends_s, saturation, slab_index, 0)
        return (pressure, saturation, ends_p, ends_s, errors)

    result = lax.fori_loop(
        0,
        sections,
        one_section,
        (start_p, start_s, zero_ends, zero_ends, jnp.zeros((batch_size,), jnp.float32)),
    )
    slab_pressure, slab_saturation = (
        lax.all_to_all(result[2], "tm", split_axis=0, concat_axis=1, tiled=True),
        lax.all_to_all(result[3], "tm", split_axis=0, concat_axis=1, tiled=True),
    )
    misfit = lax.dynamic_update_slice_in_dim(misfit, result[4], section_index * batch_size, 0)
    totals = lax.psum(misfit, ("tm", "space"))
    return (totals / (sections * REP_DEV * well_cells.shape[0]), slab_pressure, slab_saturation)


def solution(mesh):
    return jax.shard_map(
        body,
        mesh=mesh,
        in_specs=(
            P(None, "space", None, None),
            P("tm", "space", None, None),
            P("tm", "space", None, None),
            P("space", None, None),
            P("space", None, None),
            P("space", None, None),
            P(),
            P(),
            P("tm", None),
            P(None, "tm", None),
        ),
        out_specs=(P(), P("tm", None, "space", None, None), P("tm", None, "space", None, None)),
        check_vma=False,
    )
```

profile of v0, /device:TPU:0, one launch (start us, length us, event | category | flops | bytes accessed | tf_op | source)
XLA Modules:
  0.0 281.1 jit_solution(10147886916045654952)
XLA Ops:
  6.7 5.2 %all-gather = f32[4,1,32]{2,1,0:T(1,128)S(1)} all-gather(f32[1,1,32]{2,1,0:T(1,128)S(1)} %bitcast.154), channel_id=1, replica_groups=mesh['tm'=4,'space'=8] {'tm'}, dimensions={0}, use_global_device_ids=true | all-gather | bytes 640 | tf_op jit(solution)/shard_map/all_gather | solution.py:157
  13.9 8.2 %all_gather.10 = f32[4,4,32,256]{3,2,1,0:T(8,128)} all-gather(f32[1,4,32,256]{3,2,1,0:T(8,128)S(1)} %copy-done.7), channel_id=1, replica_groups=mesh['tm'=4,'space'=8] {'tm'}, dimensions={0}, use_global_device_ids=true | all-gather | bytes 655360 | tf_op jit(solution)/shard_map/all_gather | solution.py:156
  22.1 7.4 %all_gather.11 = f32[4,4,32,256]{3,2,1,0:T(8,128)S(1)} all-gather(f32[1,4,32,256]{3,2,1,0:T(8,128)S(1)} %copy-done.8), channel_id=1, replica_groups=mesh['tm'=4,'space'=8] {'tm'}, dimensions={0}, use_global_device_ids=true | all-gather | bytes 655360 | tf_op jit(solution)/shard_map/all_gather | solution.py:155
  29.6 5.2 %select_add_fusion = (f32[4,32,256]{2,1,0:T(8,128)S(1)}, pred[4,32,256]{2,1,0:T(8,128)(4,1)S(1)}, pred[4,32,256]{2,1,0:T(8,128)(4,1)S(1)}, pred[4,32,256]{2,1,0:...) fusion(f32[]{:T(128)} %bitcast.28, f32[]{:T(128)} %bitcast.27, ...), kind=kLoop, calls=%fused_computation.152 | loop fusion | flops 753664 | bytes 524320 | tf_op jit(solution)/shard_map/add | solution.py:96
  34.8 5.1 %add_multiply_fusion = f32[4,32,256]{2,1,0:T(8,128)S(1)} fusion(pred[4,32,256]{2,1,0:T(8,128)(4,1)S(1)} %get-tuple-element.474, pred[4,32,256]{2,1,0:T(8,128)(4,1)S(1)} %get-tuple-element.473, pred[4,32,256]{2,1,0:T(8,128)(4,1)S(1)} %get-tuple-element.472, pred[4,32,256]{2,1,0:T(8,128)(4,1)S(1)} %get-tuple-element.471, ...), kind=kLoop, calls=%fused_computation.153 | loop fusion | flops 524288 | bytes 393248 | tf_op jit(solution)/shard_map/mul | solution.py:100
  39.8 5.1 %select_add_fusion.1 = f32[4,32,256]{2,1,0:T(8,128)S(1)} fusion(pred[4,32,256]{2,1,0:T(8,128)(4,1)S(1)} %get-tuple-element.474, pred[4,32,256]{2,1,0:T(8,128)(4,1)S(1)} %get-tuple-element.473, pred[4,32,256]{2,1,0:T(8,128)(4,1)S(1)} %get-tuple-element.472, pred[4,32,256]{2,1,0:T(8,128)(4,1)S(1)} %get-tuple-element.471, ...), kind=kLoop, calls=%fused_computation.155 | loop fusion | flops 491520 | bytes 393248 | tf_op jit(solution)/shard_map/add | solution.py:96
  46.0 170.8 %while.24 = (s32[]{:T(128)}, f32[1,4,32,256]{3,2,1,0:T(8,128)S(1)}, f32[1,4,32,256]{3,2,1,0:T(8,128)S(1)}, f32[4,1,4,32,256]{4,3,2,1,0:T(8,128)}, f32[4,1,4,32,2...) while((s32[]{:T(128)}, f32[1,4,32,256]{3,2,1,0:T(8,128)S(1)}, ...), condition=%wide.region_3.4_spmd.clone, body=%wide.region_1.3_spmd.clone.sunk | while | flops 19529856 | bytes 16516069 | solution.py:182
  56.7 5.1 %collective-permute-start.3 = (f32[1,1,32,256]{3,2,1,0:T(8,128)S(1)}, f32[1,1,32,256]{3,2,1,0:T(8,128)S(1)}, u32[]{:S(2)}, u32[]{:S(2)}) collective-permute-start(f32[1,1,32,256]{3,2,1,0:T(8,128)S(1)} %get-tuple-element.656), channel_id=1, source_target_pairs={{0,1},{1,2},{2,3},{3,4},{4,5},{5,6},{6,7},{8,9},{9,10},{10,11},{11... | collective-permute-start | bytes 98312 | tf_op jit(solution)/shard_map/while/body/eval_jaxpr/ppermute | solution.py:19
  64.9 5.8 %collective-permute-start.5 = (f32[1,1,32,256]{3,2,1,0:T(8,128)S(1)}, f32[1,1,32,256]{3,2,1,0:T(8,128)S(1)}, u32[]{:S(2)}, u32[]{:S(2)}) collective-permute-start(f32[1,1,32,256]{3,2,1,0:T(8,128)S(1)} %get-tuple-element.658), channel_id=1, source_target_pairs={{0,1},{1,2},{2,3},{3,4},{4,5},{5,6},{6,7},{8,9},{9,10},{10,11},{11... | collective-permute-start | bytes 98312 | tf_op jit(solution)/shard_map/while/body/eval_jaxpr/ppermute | solution.py:19
  75.9 5.8 %collective-permute-start.7 = (f32[2,1,1,32,256]{4,3,2,1,0:T(8,128)S(1)}, f32[2,1,1,32,256]{4,3,2,1,0:T(8,128)S(1)}, u32[]{:S(2)}, u32[]{:S(2)}) collective-permute-start(f32[2,1,1,32,256]{4,3,2,1,0:T(8,128)S(1)} %get-tuple-element.662), channel_id=1, source_target_pairs={{0,1},{1,2},{2,3},{3,4},{4,5},{5,6},{6,7},{8,9},{9,10},{10,11},{11... | collective-permute-start | bytes 196616 | tf_op jit(solution)/shard_map/while/body/eval_jaxpr/ppermute | solution.py:19
  88.9 5.8 %collective-permute-start.1 = (f32[2,1,1,32,256]{4,3,2,1,0:T(8,128)S(1)}, f32[2,1,1,32,256]{4,3,2,1,0:T(8,128)S(1)}, u32[]{:S(2)}, u32[]{:S(2)}) collective-permute-start(f32[2,1,1,32,256]{4,3,2,1,0:T(8,128)S(1)} %get-tuple-element.644), channel_id=1, source_target_pairs={{0,1},{1,2},{2,3},{3,4},{4,5},{5,6},{6,7},{8,9},{9,10},{10,11},{11... | collective-permute-start | bytes 196616 | tf_op jit(solution)/shard_map/while/body/eval_jaxpr/ppermute | solution.py:19
  99.3 5.4 %collective-permute-start.3 = (f32[1,1,32,256]{3,2,1,0:T(8,128)S(1)}, f32[1,1,32,256]{3,2,1,0:T(8,128)S(1)}, u32[]{:S(2)}, u32[]{:S(2)}) collective-permute-start(f32[1,1,32,256]{3,2,1,0:T(8,128)S(1)} %get-tuple-element.656), channel_id=1, source_target_pairs={{0,1},{1,2},{2,3},{3,4},{4,5},{5,6},{6,7},{8,9},{9,10},{10,11},{11... | collective-permute-start | bytes 98312 | tf_op jit(solution)/shard_map/while/body/eval_jaxpr/ppermute | solution.py:19
  107.8 5.8 %collective-permute-start.5 = (f32[1,1,32,256]{3,2,1,0:T(8,128)S(1)}, f32[1,1,32,256]{3,2,1,0:T(8,128)S(1)}, u32[]{:S(2)}, u32[]{:S(2)}) collective-permute-start(f32[1,1,32,256]{3,2,1,0:T(8,128)S(1)} %get-tuple-element.658), channel_id=1, source_target_pairs={{0,1},{1,2},{2,3},{3,4},{4,5},{5,6},{6,7},{8,9},{9,10},{10,11},{11... | collective-permute-start | bytes 98312 | tf_op jit(solution)/shard_map/while/body/eval_jaxpr/ppermute | solution.py:19
  118.8 5.8 %collective-permute-start.7 = (f32[2,1,1,32,256]{4,3,2,1,0:T(8,128)S(1)}, f32[2,1,1,32,256]{4,3,2,1,0:T(8,128)S(1)}, u32[]{:S(2)}, u32[]{:S(2)}) collective-permute-start(f32[2,1,1,32,256]{4,3,2,1,0:T(8,128)S(1)} %get-tuple-element.662), channel_id=1, source_target_pairs={{0,1},{1,2},{2,3},{3,4},{4,5},{5,6},{6,7},{8,9},{9,10},{10,11},{11... | collective-permute-start | bytes 196616 | tf_op jit(solution)/shard_map/while/body/eval_jaxpr/ppermute | solution.py:19
  131.8 5.9 %collective-permute-start.1 = (f32[2,1,1,32,256]{4,3,2,1,0:T(8,128)S(1)}, f32[2,1,1,32,256]{4,3,2,1,0:T(8,128)S(1)}, u32[]{:S(2)}, u32[]{:S(2)}) collective-permute-start(f32[2,1,1,32,256]{4,3,2,1,0:T(8,128)S(1)} %get-tuple-element.644), channel_id=1, source_target_pairs={{0,1},{1,2},{2,3},{3,4},{4,5},{5,6},{6,7},{8,9},{9,10},{10,11},{11... | collective-permute-start | bytes 196616 | tf_op jit(solution)/shard_map/while/body/eval_jaxpr/ppermute | solution.py:19
  142.6 5.4 %collective-permute-start.3 = (f32[1,1,32,256]{3,2,1,0:T(8,128)S(1)}, f32[1,1,32,256]{3,2,1,0:T(8,128)S(1)}, u32[]{:S(2)}, u32[]{:S(2)}) collective-permute-start(f32[1,1,32,256]{3,2,1,0:T(8,128)S(1)} %get-tuple-element.656), channel_id=1, source_target_pairs={{0,1},{1,2},{2,3},{3,4},{4,5},{5,6},{6,7},{8,9},{9,10},{10,11},{11... | collective-permute-start | bytes 98312 | tf_op jit(solution)/shard_map/while/body/eval_jaxpr/ppermute | solution.py:19
  151.0 5.9 %collective-permute-start.5 = (f32[1,1,32,256]{3,2,1,0:T(8,128)S(1)}, f32[1,1,32,256]{3,2,1,0:T(8,128)S(1)}, u32[]{:S(2)}, u32[]{:S(2)}) collective-permute-start(f32[1,1,32,256]{3,2,1,0:T(8,128)S(1)} %get-tuple-element.658), channel_id=1, source_target_pairs={{0,1},{1,2},{2,3},{3,4},{4,5},{5,6},{6,7},{8,9},{9,10},{10,11},{11... | collective-permute-start | bytes 98312 | tf_op jit(solution)/shard_map/while/body/eval_jaxpr/ppermute | solution.py:19
  162.2 5.7 %collective-permute-start.7 = (f32[2,1,1,32,256]{4,3,2,1,0:T(8,128)S(1)}, f32[2,1,1,32,256]{4,3,2,1,0:T(8,128)S(1)}, u32[]{:S(2)}, u32[]{:S(2)}) collective-permute-start(f32[2,1,1,32,256]{4,3,2,1,0:T(8,128)S(1)} %get-tuple-element.662), channel_id=1, source_target_pairs={{0,1},{1,2},{2,3},{3,4},{4,5},{5,6},{6,7},{8,9},{9,10},{10,11},{11... | collective-permute-start | bytes 196616 | tf_op jit(solution)/shard_map/while/body/eval_jaxpr/ppermute | solution.py:19
  175.2 5.8 %collective-permute-start.1 = (f32[2,1,1,32,256]{4,3,2,1,0:T(8,128)S(1)}, f32[2,1,1,32,256]{4,3,2,1,0:T(8,128)S(1)}, u32[]{:S(2)}, u32[]{:S(2)}) collective-permute-start(f32[2,1,1,32,256]{4,3,2,1,0:T(8,128)S(1)} %get-tuple-element.644), channel_id=1, source_target_pairs={{0,1},{1,2},{2,3},{3,4},{4,5},{5,6},{6,7},{8,9},{9,10},{10,11},{11... | collective-permute-start | bytes 196616 | tf_op jit(solution)/shard_map/while/body/eval_jaxpr/ppermute | solution.py:19
  185.6 5.4 %collective-permute-start.3 = (f32[1,1,32,256]{3,2,1,0:T(8,128)S(1)}, f32[1,1,32,256]{3,2,1,0:T(8,128)S(1)}, u32[]{:S(2)}, u32[]{:S(2)}) collective-permute-start(f32[1,1,32,256]{3,2,1,0:T(8,128)S(1)} %get-tuple-element.656), channel_id=1, source_target_pairs={{0,1},{1,2},{2,3},{3,4},{4,5},{5,6},{6,7},{8,9},{9,10},{10,11},{11... | collective-permute-start | bytes 98312 | tf_op jit(solution)/shard_map/while/body/eval_jaxpr/ppermute | solution.py:19
  194.1 5.8 %collective-permute-start.5 = (f32[1,1,32,256]{3,2,1,0:T(8,128)S(1)}, f32[1,1,32,256]{3,2,1,0:T(8,128)S(1)}, u32[]{:S(2)}, u32[]{:S(2)}) collective-permute-start(f32[1,1,32,256]{3,2,1,0:T(8,128)S(1)} %get-tuple-element.658), channel_id=1, source_target_pairs={{0,1},{1,2},{2,3},{3,4},{4,5},{5,6},{6,7},{8,9},{9,10},{10,11},{11... | collective-permute-start | bytes 98312 | tf_op jit(solution)/shard_map/while/body/eval_jaxpr/ppermute | solution.py:19
  205.1 5.8 %collective-permute-start.7 = (f32[2,1,1,32,256]{4,3,2,1,0:T(8,128)S(1)}, f32[2,1,1,32,256]{4,3,2,1,0:T(8,128)S(1)}, u32[]{:S(2)}, u32[]{:S(2)}) collective-permute-start(f32[2,1,1,32,256]{4,3,2,1,0:T(8,128)S(1)} %get-tuple-element.662), channel_id=1, source_target_pairs={{0,1},{1,2},{2,3},{3,4},{4,5},{5,6},{6,7},{8,9},{9,10},{10,11},{11... | collective-permute-start | bytes 196616 | tf_op jit(solution)/shard_map/while/body/eval_jaxpr/ppermute | solution.py:19
  216.8 12.3 %all_to_all.36 = f32[4,1,4,32,256]{4,3,2,1,0:T(8,128)S(1)} all-to-all(f32[4,1,4,32,256]{4,3,2,1,0:T(8,128)} %get-tuple-element.380), channel_id=1, replica_groups=mesh['tm'=4,'space'=8] {'tm'}, dimensions={0} | all-to-all | bytes 1048576 | tf_op jit(solution)/shard_map/all_to_all | solution.py:189
  232.6 46.4 %psum.7 = f32[4]{0:T(128)S(1)} all-reduce(f32[4]{0:T(128)S(1)} %dynamic_update_slice.24), channel_id=1, replica_groups=mesh['tm'=4,'space'=8] {'tm','space'}, use_global_device_ids=true, to_apply=%region_4.5 | all-reduce | flops 4 | bytes 32 | tf_op jit(solution)/shard_map/psum | solution.py:193
  (189 shorter events, 97.1 us)
Async XLA Ops:
  0.7 44.4 %all-to-all-start = ((f32[4,1,32]{2,1,0:T(1,128)}), f32[4,1,32]{2,1,0:T(1,128)S(1)}, u32[]{:S(2)}, u32[]{:S(2)}) async-start(f32[4,1,32]{2,1,0:T(1,128)} %param.21), calls=%async_computation | async-start | bytes 4096 | tf_op jit(solution)/shard_map/all_to_all | solution.py:159
  63.6 7.1 %collective-permute-start.4 = (f32[1,1,32,256]{3,2,1,0:T(8,128)S(1)}, f32[1,1,32,256]{3,2,1,0:T(8,128)S(1)}, u32[]{:S(2)}, u32[]{:S(2)}) collective-permute-start(f32[1,1,32,256]{3,2,1,0:T(8,128)S(1)} %get-tuple-element.657), channel_id=1, source_target_pairs={{1,0},{2,1},{3,2},{4,3},{5,4},{6,5},{7,6},{9,8},{10,9},{11,10},{12... | collective-permute-start | bytes 98312 | tf_op jit(solution)/shard_map/while/body/eval_jaxpr/ppermute | solution.py:21
  64.9 7.4 %collective-permute-start.5 = (f32[1,1,32,256]{3,2,1,0:T(8,128)S(1)}, f32[1,1,32,256]{3,2,1,0:T(8,128)S(1)}, u32[]{:S(2)}, u32[]{:S(2)}) collective-permute-start(f32[1,1,32,256]{3,2,1,0:T(8,128)S(1)} %get-tuple-element.658), channel_id=1, source_target_pairs={{0,1},{1,2},{2,3},{3,4},{4,5},{5,6},{6,7},{8,9},{9,10},{10,11},{11... | collective-permute-start | bytes 98312 | tf_op jit(solution)/shard_map/while/body/eval_jaxpr/ppermute | solution.py:19
  74.4 12.0 %collective-permute-start.6 = (f32[2,1,1,32,256]{4,3,2,1,0:T(8,128)S(1)}, f32[2,1,1,32,256]{4,3,2,1,0:T(8,128)S(1)}, u32[]{:S(2)}, u32[]{:S(2)}) collective-permute-start(f32[2,1,1,32,256]{4,3,2,1,0:T(8,128)S(1)} %get-tuple-element.661), channel_id=1, source_target_pairs={{1,0},{2,1},{3,2},{4,3},{5,4},{6,5},{7,6},{9,8},{10,9},{11,10},{12... | collective-permute-start | bytes 196616 | tf_op jit(solution)/shard_map/while/body/eval_jaxpr/ppermute | solution.py:21
  75.9 10.6 %collective-permute-start.7 = (f32[2,1,1,32,256]{4,3,2,1,0:T(8,128)S(1)}, f32[2,1,1,32,256]{4,3,2,1,0:T(8,128)S(1)}, u32[]{:S(2)}, u32[]{:S(2)}) collective-permute-start(f32[2,1,1,32,256]{4,3,2,1,0:T(8,128)S(1)} %get-tuple-element.662), channel_id=1, source_target_pairs={{0,1},{1,2},{2,3},{3,4},{4,5},{5,6},{6,7},{8,9},{9,10},{10,11},{11... | collective-permute-start | bytes 196616 | tf_op jit(solution)/shard_map/while/body/eval_jaxpr/ppermute | solution.py:19
  87.6 7.4 %collective-permute-start = (f32[2,1,1,32,256]{4,3,2,1,0:T(8,128)S(1)}, f32[2,1,1,32,256]{4,3,2,1,0:T(8,128)S(1)}, u32[]{:S(2)}, u32[]{:S(2)}) collective-permute-start(f32[2,1,1,32,256]{4,3,2,1,0:T(8,128)S(1)} %get-tuple-element.643), channel_id=1, source_target_pairs={{1,0},{2,1},{3,2},{4,3},{5,4},{6,5},{7,6},{9,8},{10,9},{11,10},{12... | collective-permute-start | bytes 196616 | tf_op jit(solution)/shard_map/while/body/eval_jaxpr/ppermute | solution.py:21
  88.9 7.6 %collective-permute-start.1 = (f32[2,1,1,32,256]{4,3,2,1,0:T(8,128)S(1)}, f32[2,1,1,32,256]{4,3,2,1,0:T(8,128)S(1)}, u32[]{:S(2)}, u32[]{:S(2)}) collective-permute-start(f32[2,1,1,32,256]{4,3,2,1,0:T(8,128)S(1)} %get-tuple-element.644), channel_id=1, source_target_pairs={{0,1},{1,2},{2,3},{3,4},{4,5},{5,6},{6,7},{8,9},{9,10},{10,11},{11... | collective-permute-start | bytes 196616 | tf_op jit(solution)/shard_map/while/body/eval_jaxpr/ppermute | solution.py:19
  106.5 7.1 %collective-permute-start.4 = (f32[1,1,32,256]{3,2,1,0:T(8,128)S(1)}, f32[1,1,32,256]{3,2,1,0:T(8,128)S(1)}, u32[]{:S(2)}, u32[]{:S(2)}) collective-permute-start(f32[1,1,32,256]{3,2,1,0:T(8,128)S(1)} %get-tuple-element.657), channel_id=1, source_target_pairs={{1,0},{2,1},{3,2},{4,3},{5,4},{6,5},{7,6},{9,8},{10,9},{11,10},{12... | collective-permute-start | bytes 98312 | tf_op jit(solution)/shard_map/while/body/eval_jaxpr/ppermute | solution.py:21
  107.8 7.4 %collective-permute-start.5 = (f32[1,1,32,256]{3,2,1,0:T(8,128)S(1)}, f32[1,1,32,256]{3,2,1,0:T(8,128)S(1)}, u32[]{:S(2)}, u32[]{:S(2)}) collective-permute-start(f32[1,1,32,256]{3,2,1,0:T(8,128)S(1)} %get-tuple-element.658), channel_id=1, source_target_pairs={{0,1},{1,2},{2,3},{3,4},{4,5},{5,6},{6,7},{8,9},{9,10},{10,11},{11... | collective-permute-start | bytes 98312 | tf_op jit(solution)/shard_map/while/body/eval_jaxpr/ppermute | solution.py:19
  117.4 12.0 %collective-permute-start.6 = (f32[2,1,1,32,256]{4,3,2,1,0:T(8,128)S(1)}, f32[2,1,1,32,256]{4,3,2,1,0:T(8,128)S(1)}, u32[]{:S(2)}, u32[]{:S(2)}) collective-permute-start(f32[2,1,1,32,256]{4,3,2,1,0:T(8,128)S(1)} %get-tuple-element.661), channel_id=1, source_target_pairs={{1,0},{2,1},{3,2},{4,3},{5,4},{6,5},{7,6},{9,8},{10,9},{11,10},{12... | collective-permute-start | bytes 196616 | tf_op jit(solution)/shard_map/while/body/eval_jaxpr/ppermute | solution.py:21
  118.8 10.6 %collective-permute-start.7 = (f32[2,1,1,32,256]{4,3,2,1,0:T(8,128)S(1)}, f32[2,1,1,32,256]{4,3,2,1,0:T(8,128)S(1)}, u32[]{:S(2)}, u32[]{:S(2)}) collective-permute-start(f32[2,1,1,32,256]{4,3,2,1,0:T(8,128)S(1)} %get-tuple-element.662), channel_id=1, source_target_pairs={{0,1},{1,2},{2,3},{3,4},{4,5},{5,6},{6,7},{8,9},{9,10},{10,11},{11... | collective-permute-start | bytes 196616 | tf_op jit(solution)/shard_map/while/body/eval_jaxpr/ppermute | solution.py:19
  130.5 7.6 %collective-permute-start = (f32[2,1,1,32,256]{4,3,2,1,0:T(8,128)S(1)}, f32[2,1,1,32,256]{4,3,2,1,0:T(8,128)S(1)}, u32[]{:S(2)}, u32[]{:S(2)}) collective-permute-start(f32[2,1,1,32,256]{4,3,2,1,0:T(8,128)S(1)} %get-tuple-element.643), channel_id=1, source_target_pairs={{1,0},{2,1},{3,2},{4,3},{5,4},{6,5},{7,6},{9,8},{10,9},{11,10},{12... | collective-permute-start | bytes 196616 | tf_op jit(solution)/shard_map/while/body/eval_jaxpr/ppermute | solution.py:21
  131.8 8.0 %collective-permute-start.1 = (f32[2,1,1,32,256]{4,3,2,1,0:T(8,128)S(1)}, f32[2,1,1,32,256]{4,3,2,1,0:T(8,128)S(1)}, u32[]{:S(2)}, u32[]{:S(2)}) collective-permute-start(f32[2,1,1,32,256]{4,3,2,1,0:T(8,128)S(1)} %get-tuple-element.644), channel_id=1, source_target_pairs={{0,1},{1,2},{2,3},{3,4},{4,5},{5,6},{6,7},{8,9},{9,10},{10,11},{11... | collective-permute-start | bytes 196616 | tf_op jit(solution)/shard_map/while/body/eval_jaxpr/ppermute | solution.py:19
  149.7 7.3 %collective-permute-start.4 = (f32[1,1,32,256]{3,2,1,0:T(8,128)S(1)}, f32[1,1,32,256]{3,2,1,0:T(8,128)S(1)}, u32[]{:S(2)}, u32[]{:S(2)}) collective-permute-start(f32[1,1,32,256]{3,2,1,0:T(8,128)S(1)} %get-tuple-element.657), channel_id=1, source_target_pairs={{1,0},{2,1},{3,2},{4,3},{5,4},{6,5},{7,6},{9,8},{10,9},{11,10},{12... | collective-permute-start | bytes 98312 | tf_op jit(solution)/shard_map/while/body/eval_jaxpr/ppermute | solution.py:21
  151.0 7.6 %collective-permute-start.5 = (f32[1,1,32,256]{3,2,1,0:T(8,128)S(1)}, f32[1,1,32,256]{3,2,1,0:T(8,128)S(1)}, u32[]{:S(2)}, u32[]{:S(2)}) collective-permute-start(f32[1,1,32,256]{3,2,1,0:T(8,128)S(1)} %get-tuple-element.658), channel_id=1, source_target_pairs={{0,1},{1,2},{2,3},{3,4},{4,5},{5,6},{6,7},{8,9},{9,10},{10,11},{11... | collective-permute-start | bytes 98312 | tf_op jit(solution)/shard_map/while/body/eval_jaxpr/ppermute | solution.py:19
  160.8 12.0 %collective-permute-start.6 = (f32[2,1,1,32,256]{4,3,2,1,0:T(8,128)S(1)}, f32[2,1,1,32,256]{4,3,2,1,0:T(8,128)S(1)}, u32[]{:S(2)}, u32[]{:S(2)}) collective-permute-start(f32[2,1,1,32,256]{4,3,2,1,0:T(8,128)S(1)} %get-tuple-element.661), channel_id=1, source_target_pairs={{1,0},{2,1},{3,2},{4,3},{5,4},{6,5},{7,6},{9,8},{10,9},{11,10},{12... | collective-permute-start | bytes 196616 | tf_op jit(solution)/shard_map/while/body/eval_jaxpr/ppermute | solution.py:21
  162.2 10.5 %collective-permute-start.7 = (f32[2,1,1,32,256]{4,3,2,1,0:T(8,128)S(1)}, f32[2,1,1,32,256]{4,3,2,1,0:T(8,128)S(1)}, u32[]{:S(2)}, u32[]{:S(2)}) collective-permute-start(f32[2,1,1,32,256]{4,3,2,1,0:T(8,128)S(1)} %get-tuple-element.662), channel_id=1, source_target_pairs={{0,1},{1,2},{2,3},{3,4},{4,5},{5,6},{6,7},{8,9},{9,10},{10,11},{11... | collective-permute-start | bytes 196616 | tf_op jit(solution)/shard_map/while/body/eval_jaxpr/ppermute | solution.py:19
  173.9 7.4 %collective-permute-start = (f32[2,1,1,32,256]{4,3,2,1,0:T(8,128)S(1)}, f32[2,1,1,32,256]{4,3,2,1,0:T(8,128)S(1)}, u32[]{:S(2)}, u32[]{:S(2)}) collective-permute-start(f32[2,1,1,32,256]{4,3,2,1,0:T(8,128)S(1)} %get-tuple-element.643), channel_id=1, source_target_pairs={{1,0},{2,1},{3,2},{4,3},{5,4},{6,5},{7,6},{9,8},{10,9},{11,10},{12... | collective-permute-start | bytes 196616 | tf_op jit(solution)/shard_map/while/body/eval_jaxpr/ppermute | solution.py:21
  175.2 7.6 %collective-permute-start.1 = (f32[2,1,1,32,256]{4,3,2,1,0:T(8,128)S(1)}, f32[2,1,1,32,256]{4,3,2,1,0:T(8,128)S(1)}, u32[]{:S(2)}, u32[]{:S(2)}) collective-permute-start(f32[2,1,1,32,256]{4,3,2,1,0:T(8,128)S(1)} %get-tuple-element.644), channel_id=1, source_target_pairs={{0,1},{1,2},{2,3},{3,4},{4,5},{5,6},{6,7},{8,9},{9,10},{10,11},{11... | collective-permute-start | bytes 196616 | tf_op jit(solution)/shard_map/while/body/eval_jaxpr/ppermute | solution.py:19
  192.8 7.1 %collective-permute-start.4 = (f32[1,1,32,256]{3,2,1,0:T(8,128)S(1)}, f32[1,1,32,256]{3,2,1,0:T(8,128)S(1)}, u32[]{:S(2)}, u32[]{:S(2)}) collective-permute-start(f32[1,1,32,256]{3,2,1,0:T(8,128)S(1)} %get-tuple-element.657), channel_id=1, source_target_pairs={{1,0},{2,1},{3,2},{4,3},{5,4},{6,5},{7,6},{9,8},{10,9},{11,10},{12... | collective-permute-start | bytes 98312 | tf_op jit(solution)/shard_map/while/body/eval_jaxpr/ppermute | solution.py:21
  194.1 7.4 %collective-permute-start.5 = (f32[1,1,32,256]{3,2,1,0:T(8,128)S(1)}, f32[1,1,32,256]{3,2,1,0:T(8,128)S(1)}, u32[]{:S(2)}, u32[]{:S(2)}) collective-permute-start(f32[1,1,32,256]{3,2,1,0:T(8,128)S(1)} %get-tuple-element.658), channel_id=1, source_target_pairs={{0,1},{1,2},{2,3},{3,4},{4,5},{5,6},{6,7},{8,9},{9,10},{10,11},{11... | collective-permute-start | bytes 98312 | tf_op jit(solution)/shard_map/while/body/eval_jaxpr/ppermute | solution.py:19
  203.7 12.0 %collective-permute-start.6 = (f32[2,1,1,32,256]{4,3,2,1,0:T(8,128)S(1)}, f32[2,1,1,32,256]{4,3,2,1,0:T(8,128)S(1)}, u32[]{:S(2)}, u32[]{:S(2)}) collective-permute-start(f32[2,1,1,32,256]{4,3,2,1,0:T(8,128)S(1)} %get-tuple-element.661), channel_id=1, source_target_pairs={{1,0},{2,1},{3,2},{4,3},{5,4},{6,5},{7,6},{9,8},{10,9},{11,10},{12... | collective-permute-start | bytes 196616 | tf_op jit(solution)/shard_map/while/body/eval_jaxpr/ppermute | solution.py:21
  205.1 10.6 %collective-permute-start.7 = (f32[2,1,1,32,256]{4,3,2,1,0:T(8,128)S(1)}, f32[2,1,1,32,256]{4,3,2,1,0:T(8,128)S(1)}, u32[]{:S(2)}, u32[]{:S(2)}) collective-permute-start(f32[2,1,1,32,256]{4,3,2,1,0:T(8,128)S(1)} %get-tuple-element.662), channel_id=1, source_target_pairs={{0,1},{1,2},{2,3},{3,4},{4,5},{5,6},{6,7},{8,9},{9,10},{10,11},{11... | collective-permute-start | bytes 196616 | tf_op jit(solution)/shard_map/while/body/eval_jaxpr/ppermute | solution.py:19
  229.0 50.5 %all-to-all-start.2 = ((f32[4,1,4,32,256]{4,3,2,1,0:T(8,128)}), f32[4,1,4,32,256]{4,3,2,1,0:T(8,128)S(1)}, u32[]{:S(2)}, u32[]{:S(2)}) async-start(f32[4,1,4,32,256]{4,3,2,1,0:T(8,128)} %get-tuple-element.381), calls=%async_computation.2 | async-start | bytes 1048576 | tf_op jit(solution)/shard_map/all_to_all | solution.py:190
  (32 other events, 182.1 us)
where the time goes:
time: 283 us; the launch traced here: 281 us
  starting transfers between devices  119 us (42%)
  blocking collectives  79.4 us (28%)
  other arithmetic  33.1 us (12%)
  waiting for transfers between devices  20.6 us (7%)
  matrix products  17.5 us (6%)
  local copies, waits for them, and re-layouts  7.58 us (3%)
  loops' own time  3.42 us (1%)
    ppermute x16, starting transfers between devices, padded(): lax.ppermute(tail, axis, [(i, (i + 1) % count) for i in range(ends)])  89.6 us
    psum x1, blocking collectives, body(): totals = lax.psum(misfit, ('tm', 'space'))  46.4 us
    ppermute x16, starting transfers between devices, padded(): lax.ppermute(head, axis, [((i + 1) % count, i) for i in range(ends)])  21.2 us
    ppermute x16, waiting for transfers between devices, padded(): lax.ppermute(tail, axis, [(i, (i + 1) % count) for i in range(ends)])  18.9 us
    dot_general x4, matrix products, mismatch(): jnp.dot(pressure.reshape(batch_size, -1), well_picks.T, precision=lax.Pre...  16.2 us
    all_to_all x1, blocking collectives, body(): lax.all_to_all(result[2], 'tm', split_axis=0, concat_axis=1, tiled=True)  12.3 us
    add x2, other arithmetic, region_fields(): summed + jnp.where(region_ids == region_index, region_table[table_row, re...  10.3 us
    all_gather x1, blocking collectives, body(): lax.all_gather(inflow, 'tm', axis=0, tiled=True)  8.19 us
  transfers between devices with their start and end apart: 34, of which 17 were waited for; matrix products, arithmetic and copies ran while one was open for 13% of the time, Pallas kernels for 0%

commit v1 on v0

--- a/solution.py
+++ b/solution.py
@@ -190,7 +190,7 @@
         lax.all_to_all(result[3], "tm", split_axis=0, concat_axis=1, tiled=True),
     )
     misfit = lax.dynamic_update_slice_in_dim(misfit, result[4], section_index * batch_size, 0)
-    totals = lax.psum(misfit, ("tm", "space"))
+    totals = lax.psum(lax.psum(misfit, "tm"), "space")
     return (totals / (sections * REP_DEV * well_cells.shape[0]), slab_pressure, slab_saturation)
 
 

time: 283 us -> 270 us (0.954)
  blocking collectives: 79.4 us -> 67.2 us
    psum x1 -> x2, blocking collectives: 46.4 us -> 34.2 us  [body(): totals = lax.psum(lax.psum(misfit, 'tm'), 'space')]
  transfers between devices with their start and end apart: 34 -> 34, of which waited for: 17 -> 17; matrix products, arithmetic and copies ran while one was open for 13% -> 14% of each run, Pallas kernels for 0% -> 0%
where the time goes in v1:
time: 270 us; the launch traced here: 268 us
  starting transfers between devices  119 us (44%)
  blocking collectives  67.2 us (25%)
  other arithmetic  33.2 us (12%)
  waiting for transfers between devices  20.6 us (8%)
  matrix products  17.3 us (6%)
  local copies, waits for them, and re-layouts  7.57 us (3%)
  loops' own time  3.16 us (1%)
    ppermute x16, starting transfers between devices, padded(): lax.ppermute(tail, axis, [(i, (i + 1) % count) for i in range(ends)])  89.6 us
    psum x2, blocking collectives, body(): totals = lax.psum(lax.psum(misfit, 'tm'), 'space')  34.2 us
    ppermute x16, starting transfers between devices, padded(): lax.ppermute(head, axis, [((i + 1) % count, i) for i in range(ends)])  21.2 us
    ppermute x16, waiting for transfers between devices, padded(): lax.ppermute(tail, axis, [(i, (i + 1) % count) for i in range(ends)])  18.9 us
    dot_general x4, matrix products, mismatch(): jnp.dot(pressure.reshape(batch_size, -1), well_picks.T, precision=lax.Pre...  16 us
    all_to_all x1, blocking collectives, body(): lax.all_to_all(result[2], 'tm', split_axis=0, concat_axis=1, tiled=True)  12.3 us
    add x2, other arithmetic, region_fields(): summed + jnp.where(region_ids == region_index, region_table[table_row, re...  10.3 us
    all_gather x1, blocking collectives, body(): lax.all_gather(inflow, 'tm', axis=0, tiled=True)  8.19 us
  transfers between devices with their start and end apart: 34, of which 17 were waited for; matrix products, arithmetic and copies ran while one was open for 14% of the time, Pallas kernels for 0%

profile of v1, /device:TPU:0, one launch (start us, length us, event | category | flops | bytes accessed | tf_op | source)
XLA Modules:
  0.0 268.5 jit_solution(4870686775482800667)
XLA Ops:
  6.6 5.2 %all-gather = f32[4,1,32]{2,1,0:T(1,128)S(1)} all-gather(f32[1,1,32]{2,1,0:T(1,128)S(1)} %bitcast.154), channel_id=1, replica_groups=mesh['tm'=4,'space'=8] {'tm'}, dimensions={0}, use_global_device_ids=true | all-gather | bytes 640 | tf_op jit(solution)/shard_map/all_gather | solution.py:157
  13.9 8.2 %all_gather.10 = f32[4,4,32,256]{3,2,1,0:T(8,128)} all-gather(f32[1,4,32,256]{3,2,1,0:T(8,128)S(1)} %copy-done.7), channel_id=1, replica_groups=mesh['tm'=4,'space'=8] {'tm'}, dimensions={0}, use_global_device_ids=true | all-gather | bytes 655360 | tf_op jit(solution)/shard_map/all_gather | solution.py:156
  22.1 7.4 %all_gather.11 = f32[4,4,32,256]{3,2,1,0:T(8,128)S(1)} all-gather(f32[1,4,32,256]{3,2,1,0:T(8,128)S(1)} %copy-done.8), channel_id=1, replica_groups=mesh['tm'=4,'space'=8] {'tm'}, dimensions={0}, use_global_device_ids=true | all-gather | bytes 655360 | tf_op jit(solution)/shard_map/all_gather | solution.py:155
  29.6 5.2 %select_add_fusion = (f32[4,32,256]{2,1,0:T(8,128)S(1)}, pred[4,32,256]{2,1,0:T(8,128)(4,1)S(1)}, pred[4,32,256]{2,1,0:T(8,128)(4,1)S(1)}, pred[4,32,256]{2,1,0:...) fusion(f32[]{:T(128)} %bitcast.28, f32[]{:T(128)} %bitcast.27, ...), kind=kLoop, calls=%fused_computation.152 | loop fusion | flops 753664 | bytes 524320 | tf_op jit(solution)/shard_map/add | solution.py:96
  34.8 5.1 %add_multiply_fusion = f32[4,32,256]{2,1,0:T(8,128)S(1)} fusion(pred[4,32,256]{2,1,0:T(8,128)(4,1)S(1)} %get-tuple-element.474, pred[4,32,256]{2,1,0:T(8,128)(4,1)S(1)} %get-tuple-element.473, pred[4,32,256]{2,1,0:T(8,128)(4,1)S(1)} %get-tuple-element.472, pred[4,32,256]{2,1,0:T(8,128)(4,1)S(1)} %get-tuple-element.471, ...), kind=kLoop, calls=%fused_computation.153 | loop fusion | flops 524288 | bytes 393248 | tf_op jit(solution)/shard_map/mul | solution.py:100
  39.9 5.1 %select_add_fusion.1 = f32[4,32,256]{2,1,0:T(8,128)S(1)} fusion(pred[4,32,256]{2,1,0:T(8,128)(4,1)S(1)} %get-tuple-element.474, pred[4,32,256]{2,1,0:T(8,128)(4,1)S(1)} %get-tuple-element.473, pred[4,32,256]{2,1,0:T(8,128)(4,1)S(1)} %get-tuple-element.472, pred[4,32,256]{2,1,0:T(8,128)(4,1)S(1)} %get-tuple-element.471, ...), kind=kLoop, calls=%fused_computation.155 | loop fusion | flops 491520 | bytes 393248 | tf_op jit(solution)/shard_map/add | solution.py:96
  46.0 170.3 %while.24 = (s32[]{:T(128)}, f32[1,4,32,256]{3,2,1,0:T(8,128)S(1)}, f32[1,4,32,256]{3,2,1,0:T(8,128)S(1)}, f32[4,1,4,32,256]{4,3,2,1,0:T(8,128)}, f32[4,1,4,32,2...) while((s32[]{:T(128)}, f32[1,4,32,256]{3,2,1,0:T(8,128)S(1)}, ...), condition=%wide.region_3.4_spmd.clone, body=%wide.region_1.3_spmd.clone.sunk | while | flops 19529856 | bytes 16516069 | solution.py:182
  64.9 5.8 %collective-permute-start.5 = (f32[1,1,32,256]{3,2,1,0:T(8,128)S(1)}, f32[1,1,32,256]{3,2,1,0:T(8,128)S(1)}, u32[]{:S(2)}, u32[]{:S(2)}) collective-permute-start(f32[1,1,32,256]{3,2,1,0:T(8,128)S(1)} %get-tuple-element.658), channel_id=1, source_target_pairs={{0,1},{1,2},{2,3},{3,4},{4,5},{5,6},{6,7},{8,9},{9,10},{10,11},{11... | collective-permute-start | bytes 98312 | tf_op jit(solution)/shard_map/while/body/eval_jaxpr/ppermute | solution.py:19
  75.9 5.8 %collective-permute-start.7 = (f32[2,1,1,32,256]{4,3,2,1,0:T(8,128)S(1)}, f32[2,1,1,32,256]{4,3,2,1,0:T(8,128)S(1)}, u32[]{:S(2)}, u32[]{:S(2)}) collective-permute-start(f32[2,1,1,32,256]{4,3,2,1,0:T(8,128)S(1)} %get-tuple-element.662), channel_id=1, source_target_pairs={{0,1},{1,2},{2,3},{3,4},{4,5},{5,6},{6,7},{8,9},{9,10},{10,11},{11... | collective-permute-start | bytes 196616 | tf_op jit(solution)/shard_map/while/body/eval_jaxpr/ppermute | solution.py:19
  88.8 5.8 %collective-permute-start.1 = (f32[2,1,1,32,256]{4,3,2,1,0:T(8,128)S(1)}, f32[2,1,1,32,256]{4,3,2,1,0:T(8,128)S(1)}, u32[]{:S(2)}, u32[]{:S(2)}) collective-permute-start(f32[2,1,1,32,256]{4,3,2,1,0:T(8,128)S(1)} %get-tuple-element.644), channel_id=1, source_target_pairs={{0,1},{1,2},{2,3},{3,4},{4,5},{5,6},{6,7},{8,9},{9,10},{10,11},{11... | collective-permute-start | bytes 196616 | tf_op jit(solution)/shard_map/while/body/eval_jaxpr/ppermute | solution.py:19
  99.2 5.4 %collective-permute-start.3 = (f32[1,1,32,256]{3,2,1,0:T(8,128)S(1)}, f32[1,1,32,256]{3,2,1,0:T(8,128)S(1)}, u32[]{:S(2)}, u32[]{:S(2)}) collective-permute-start(f32[1,1,32,256]{3,2,1,0:T(8,128)S(1)} %get-tuple-element.656), channel_id=1, source_target_pairs={{0,1},{1,2},{2,3},{3,4},{4,5},{5,6},{6,7},{8,9},{9,10},{10,11},{11... | collective-permute-start | bytes 98312 | tf_op jit(solution)/shard_map/while/body/eval_jaxpr/ppermute | solution.py:19
  107.7 5.8 %collective-permute-start.5 = (f32[1,1,32,256]{3,2,1,0:T(8,128)S(1)}, f32[1,1,32,256]{3,2,1,0:T(8,128)S(1)}, u32[]{:S(2)}, u32[]{:S(2)}) collective-permute-start(f32[1,1,32,256]{3,2,1,0:T(8,128)S(1)} %get-tuple-element.658), channel_id=1, source_target_pairs={{0,1},{1,2},{2,3},{3,4},{4,5},{5,6},{6,7},{8,9},{9,10},{10,11},{11... | collective-permute-start | bytes 98312 | tf_op jit(solution)/shard_map/while/body/eval_jaxpr/ppermute | solution.py:19
  118.7 5.8 %collective-permute-start.7 = (f32[2,1,1,32,256]{4,3,2,1,0:T(8,128)S(1)}, f32[2,1,1,32,256]{4,3,2,1,0:T(8,128)S(1)}, u32[]{:S(2)}, u32[]{:S(2)}) collective-permute-start(f32[2,1,1,32,256]{4,3,2,1,0:T(8,128)S(1)} %get-tuple-element.662), channel_id=1, source_target_pairs={{0,1},{1,2},{2,3},{3,4},{4,5},{5,6},{6,7},{8,9},{9,10},{10,11},{11... | collective-permute-start | bytes 196616 | tf_op jit(solution)/shard_map/while/body/eval_jaxpr/ppermute | solution.py:19
  131.7 5.9 %collective-permute-start.1 = (f32[2,1,1,32,256]{4,3,2,1,0:T(8,128)S(1)}, f32[2,1,1,32,256]{4,3,2,1,0:T(8,128)S(1)}, u32[]{:S(2)}, u32[]{:S(2)}) collective-permute-start(f32[2,1,1,32,256]{4,3,2,1,0:T(8,128)S(1)} %get-tuple-element.644), channel_id=1, source_target_pairs={{0,1},{1,2},{2,3},{3,4},{4,5},{5,6},{6,7},{8,9},{9,10},{10,11},{11... | collective-permute-start | bytes 196616 | tf_op jit(solution)/shard_map/while/body/eval_jaxpr/ppermute | solution.py:19
  142.4 5.4 %collective-permute-start.3 = (f32[1,1,32,256]{3,2,1,0:T(8,128)S(1)}, f32[1,1,32,256]{3,2,1,0:T(8,128)S(1)}, u32[]{:S(2)}, u32[]{:S(2)}) collective-permute-start(f32[1,1,32,256]{3,2,1,0:T(8,128)S(1)} %get-tuple-element.656), channel_id=1, source_target_pairs={{0,1},{1,2},{2,3},{3,4},{4,5},{5,6},{6,7},{8,9},{9,10},{10,11},{11... | collective-permute-start | bytes 98312 | tf_op jit(solution)/shard_map/while/body/eval_jaxpr/ppermute | solution.py:19
  150.9 5.9 %collective-permute-start.5 = (f32[1,1,32,256]{3,2,1,0:T(8,128)S(1)}, f32[1,1,32,256]{3,2,1,0:T(8,128)S(1)}, u32[]{:S(2)}, u32[]{:S(2)}) collective-permute-start(f32[1,1,32,256]{3,2,1,0:T(8,128)S(1)} %get-tuple-element.658), channel_id=1, source_target_pairs={{0,1},{1,2},{2,3},{3,4},{4,5},{5,6},{6,7},{8,9},{9,10},{10,11},{11... | collective-permute-start | bytes 98312 | tf_op jit(solution)/shard_map/while/body/eval_jaxpr/ppermute | solution.py:19
  162.1 5.7 %collective-permute-start.7 = (f32[2,1,1,32,256]{4,3,2,1,0:T(8,128)S(1)}, f32[2,1,1,32,256]{4,3,2,1,0:T(8,128)S(1)}, u32[]{:S(2)}, u32[]{:S(2)}) collective-permute-start(f32[2,1,1,32,256]{4,3,2,1,0:T(8,128)S(1)} %get-tuple-element.662), channel_id=1, source_target_pairs={{0,1},{1,2},{2,3},{3,4},{4,5},{5,6},{6,7},{8,9},{9,10},{10,11},{11... | collective-permute-start | bytes 196616 | tf_op jit(solution)/shard_map/while/body/eval_jaxpr/ppermute | solution.py:19
  174.9 5.8 %collective-permute-start.1 = (f32[2,1,1,32,256]{4,3,2,1,0:T(8,128)S(1)}, f32[2,1,1,32,256]{4,3,2,1,0:T(8,128)S(1)}, u32[]{:S(2)}, u32[]{:S(2)}) collective-permute-start(f32[2,1,1,32,256]{4,3,2,1,0:T(8,128)S(1)} %get-tuple-element.644), channel_id=1, source_target_pairs={{0,1},{1,2},{2,3},{3,4},{4,5},{5,6},{6,7},{8,9},{9,10},{10,11},{11... | collective-permute-start | bytes 196616 | tf_op jit(solution)/shard_map/while/body/eval_jaxpr/ppermute | solution.py:19
  185.3 5.4 %collective-permute-start.3 = (f32[1,1,32,256]{3,2,1,0:T(8,128)S(1)}, f32[1,1,32,256]{3,2,1,0:T(8,128)S(1)}, u32[]{:S(2)}, u32[]{:S(2)}) collective-permute-start(f32[1,1,32,256]{3,2,1,0:T(8,128)S(1)} %get-tuple-element.656), channel_id=1, source_target_pairs={{0,1},{1,2},{2,3},{3,4},{4,5},{5,6},{6,7},{8,9},{9,10},{10,11},{11... | collective-permute-start | bytes 98312 | tf_op jit(solution)/shard_map/while/body/eval_jaxpr/ppermute | solution.py:19
  193.8 5.8 %collective-permute-start.5 = (f32[1,1,32,256]{3,2,1,0:T(8,128)S(1)}, f32[1,1,32,256]{3,2,1,0:T(8,128)S(1)}, u32[]{:S(2)}, u32[]{:S(2)}) collective-permute-start(f32[1,1,32,256]{3,2,1,0:T(8,128)S(1)} %get-tuple-element.658), channel_id=1, source_target_pairs={{0,1},{1,2},{2,3},{3,4},{4,5},{5,6},{6,7},{8,9},{9,10},{10,11},{11... | collective-permute-start | bytes 98312 | tf_op jit(solution)/shard_map/while/body/eval_jaxpr/ppermute | solution.py:19
  204.8 5.8 %collective-permute-start.7 = (f32[2,1,1,32,256]{4,3,2,1,0:T(8,128)S(1)}, f32[2,1,1,32,256]{4,3,2,1,0:T(8,128)S(1)}, u32[]{:S(2)}, u32[]{:S(2)}) collective-permute-start(f32[2,1,1,32,256]{4,3,2,1,0:T(8,128)S(1)} %get-tuple-element.662), channel_id=1, source_target_pairs={{0,1},{1,2},{2,3},{3,4},{4,5},{5,6},{6,7},{8,9},{9,10},{10,11},{11... | collective-permute-start | bytes 196616 | tf_op jit(solution)/shard_map/while/body/eval_jaxpr/ppermute | solution.py:19
  216.3 12.3 %all_to_all.36 = f32[4,1,4,32,256]{4,3,2,1,0:T(8,128)S(1)} all-to-all(f32[4,1,4,32,256]{4,3,2,1,0:T(8,128)} %get-tuple-element.380), channel_id=1, replica_groups=mesh['tm'=4,'space'=8] {'tm'}, dimensions={0} | all-to-all | bytes 1048576 | tf_op jit(solution)/shard_map/all_to_all | solution.py:189
  232.2 10.1 %psum.14 = f32[4]{0:T(128)S(1)} all-reduce(f32[4]{0:T(128)S(1)} %dynamic_update_slice.24), channel_id=1, replica_groups=mesh['tm'=4,'space'=8] {'tm'}, use_global_device_ids=true, to_apply=%region_4.5 | all-reduce | flops 4 | bytes 32 | tf_op jit(solution)/shard_map/psum | solution.py:193
  242.3 24.0 %psum.15 = f32[4]{0:T(128)S(1)} all-reduce(f32[4]{0:T(128)S(1)} %psum.14), channel_id=1, replica_groups=mesh['tm'=4,'space'=8] {'space'}, use_global_device_ids=true, to_apply=%region_5.6 | all-reduce | flops 4 | bytes 32 | tf_op jit(solution)/shard_map/psum | solution.py:193
  (190 shorter events, 102.0 us)
Async XLA Ops:
  0.7 44.5 %all-to-all-start = ((f32[4,1,32]{2,1,0:T(1,128)}), f32[4,1,32]{2,1,0:T(1,128)S(1)}, u32[]{:S(2)}, u32[]{:S(2)}) async-start(f32[4,1,32]{2,1,0:T(1,128)} %param.21), calls=%async_computation | async-start | bytes 4096 | tf_op jit(solution)/shard_map/all_to_all | solution.py:159
  63.6 7.1 %collective-permute-start.4 = (f32[1,1,32,256]{3,2,1,0:T(8,128)S(1)}, f32[1,1,32,256]{3,2,1,0:T(8,128)S(1)}, u32[]{:S(2)}, u32[]{:S(2)}) collective-permute-start(f32[1,1,32,256]{3,2,1,0:T(8,128)S(1)} %get-tuple-element.657), channel_id=1, source_target_pairs={{1,0},{2,1},{3,2},{4,3},{5,4},{6,5},{7,6},{9,8},{10,9},{11,10},{12... | collective-permute-start | bytes 98312 | tf_op jit(solution)/shard_map/while/body/eval_jaxpr/ppermute | solution.py:21
  64.9 7.4 %collective-permute-start.5 = (f32[1,1,32,256]{3,2,1,0:T(8,128)S(1)}, f32[1,1,32,256]{3,2,1,0:T(8,128)S(1)}, u32[]{:S(2)}, u32[]{:S(2)}) collective-permute-start(f32[1,1,32,256]{3,2,1,0:T(8,128)S(1)} %get-tuple-element.658), channel_id=1, source_target_pairs={{0,1},{1,2},{2,3},{3,4},{4,5},{5,6},{6,7},{8,9},{9,10},{10,11},{11... | collective-permute-start | bytes 98312 | tf_op jit(solution)/shard_map/while/body/eval_jaxpr/ppermute | solution.py:19
  74.5 11.9 %collective-permute-start.6 = (f32[2,1,1,32,256]{4,3,2,1,0:T(8,128)S(1)}, f32[2,1,1,32,256]{4,3,2,1,0:T(8,128)S(1)}, u32[]{:S(2)}, u32[]{:S(2)}) collective-permute-start(f32[2,1,1,32,256]{4,3,2,1,0:T(8,128)S(1)} %get-tuple-element.661), channel_id=1, source_target_pairs={{1,0},{2,1},{3,2},{4,3},{5,4},{6,5},{7,6},{9,8},{10,9},{11,10},{12... | collective-permute-start | bytes 196616 | tf_op jit(solution)/shard_map/while/body/eval_jaxpr/ppermute | solution.py:21
  75.9 10.5 %collective-permute-start.7 = (f32[2,1,1,32,256]{4,3,2,1,0:T(8,128)S(1)}, f32[2,1,1,32,256]{4,3,2,1,0:T(8,128)S(1)}, u32[]{:S(2)}, u32[]{:S(2)}) collective-permute-start(f32[2,1,1,32,256]{4,3,2,1,0:T(8,128)S(1)} %get-tuple-element.662), channel_id=1, source_target_pairs={{0,1},{1,2},{2,3},{3,4},{4,5},{5,6},{6,7},{8,9},{9,10},{10,11},{11... | collective-permute-start | bytes 196616 | tf_op jit(solution)/shard_map/while/body/eval_jaxpr/ppermute | solution.py:19
  87.5 7.4 %collective-permute-start = (f32[2,1,1,32,256]{4,3,2,1,0:T(8,128)S(1)}, f32[2,1,1,32,256]{4,3,2,1,0:T(8,128)S(1)}, u32[]{:S(2)}, u32[]{:S(2)}) collective-permute-start(f32[2,1,1,32,256]{4,3,2,1,0:T(8,128)S(1)} %get-tuple-element.643), channel_id=1, source_target_pairs={{1,0},{2,1},{3,2},{4,3},{5,4},{6,5},{7,6},{9,8},{10,9},{11,10},{12... | collective-permute-start | bytes 196616 | tf_op jit(solution)/shard_map/while/body/eval_jaxpr/ppermute | solution.py:21
  88.8 7.6 %collective-permute-start.1 = (f32[2,1,1,32,256]{4,3,2,1,0:T(8,128)S(1)}, f32[2,1,1,32,256]{4,3,2,1,0:T(8,128)S(1)}, u32[]{:S(2)}, u32[]{:S(2)}) collective-permute-start(f32[2,1,1,32,256]{4,3,2,1,0:T(8,128)S(1)} %get-tuple-element.644), channel_id=1, source_target_pairs={{0,1},{1,2},{2,3},{3,4},{4,5},{5,6},{6,7},{8,9},{9,10},{10,11},{11... | collective-permute-start | bytes 196616 | tf_op jit(solution)/shard_map/while/body/eval_jaxpr/ppermute | solution.py:19
  106.4 7.1 %collective-permute-start.4 = (f32[1,1,32,256]{3,2,1,0:T(8,128)S(1)}, f32[1,1,32,256]{3,2,1,0:T(8,128)S(1)}, u32[]{:S(2)}, u32[]{:S(2)}) collective-permute-start(f32[1,1,32,256]{3,2,1,0:T(8,128)S(1)} %get-tuple-element.657), channel_id=1, source_target_pairs={{1,0},{2,1},{3,2},{4,3},{5,4},{6,5},{7,6},{9,8},{10,9},{11,10},{12... | collective-permute-start | bytes 98312 | tf_op jit(solution)/shard_map/while/body/eval_jaxpr/ppermute | solution.py:21
  107.7 7.4 %collective-permute-start.5 = (f32[1,1,32,256]{3,2,1,0:T(8,128)S(1)}, f32[1,1,32,256]{3,2,1,0:T(8,128)S(1)}, u32[]{:S(2)}, u32[]{:S(2)}) collective-permute-start(f32[1,1,32,256]{3,2,1,0:T(8,128)S(1)} %get-tuple-element.658), channel_id=1, source_target_pairs={{0,1},{1,2},{2,3},{3,4},{4,5},{5,6},{6,7},{8,9},{9,10},{10,11},{11... | collective-permute-start | bytes 98312 | tf_op jit(solution)/shard_map/while/body/eval_jaxpr/ppermute | solution.py:19
  117.3 11.9 %collective-permute-start.6 = (f32[2,1,1,32,256]{4,3,2,1,0:T(8,128)S(1)}, f32[2,1,1,32,256]{4,3,2,1,0:T(8,128)S(1)}, u32[]{:S(2)}, u32[]{:S(2)}) collective-permute-start(f32[2,1,1,32,256]{4,3,2,1,0:T(8,128)S(1)} %get-tuple-element.661), channel_id=1, source_target_pairs={{1,0},{2,1},{3,2},{4,3},{5,4},{6,5},{7,6},{9,8},{10,9},{11,10},{12... | collective-permute-start | bytes 196616 | tf_op jit(solution)/shard_map/while/body/eval_jaxpr/ppermute | solution.py:21
  118.7 10.5 %collective-permute-start.7 = (f32[2,1,1,32,256]{4,3,2,1,0:T(8,128)S(1)}, f32[2,1,1,32,256]{4,3,2,1,0:T(8,128)S(1)}, u32[]{:S(2)}, u32[]{:S(2)}) collective-permute-start(f32[2,1,1,32,256]{4,3,2,1,0:T(8,128)S(1)} %get-tuple-element.662), channel_id=1, source_target_pairs={{0,1},{1,2},{2,3},{3,4},{4,5},{5,6},{6,7},{8,9},{9,10},{10,11},{11... | collective-permute-start | bytes 196616 | tf_op jit(solution)/shard_map/while/body/eval_jaxpr/ppermute | solution.py:19
  130.3 7.6 %collective-permute-start = (f32[2,1,1,32,256]{4,3,2,1,0:T(8,128)S(1)}, f32[2,1,1,32,256]{4,3,2,1,0:T(8,128)S(1)}, u32[]{:S(2)}, u32[]{:S(2)}) collective-permute-start(f32[2,1,1,32,256]{4,3,2,1,0:T(8,128)S(1)} %get-tuple-element.643), channel_id=1, source_target_pairs={{1,0},{2,1},{3,2},{4,3},{5,4},{6,5},{7,6},{9,8},{10,9},{11,10},{12... | collective-permute-start | bytes 196616 | tf_op jit(solution)/shard_map/while/body/eval_jaxpr/ppermute | solution.py:21
  131.7 8.0 %collective-permute-start.1 = (f32[2,1,1,32,256]{4,3,2,1,0:T(8,128)S(1)}, f32[2,1,1,32,256]{4,3,2,1,0:T(8,128)S(1)}, u32[]{:S(2)}, u32[]{:S(2)}) collective-permute-start(f32[2,1,1,32,256]{4,3,2,1,0:T(8,128)S(1)} %get-tuple-element.644), channel_id=1, source_target_pairs={{0,1},{1,2},{2,3},{3,4},{4,5},{5,6},{6,7},{8,9},{9,10},{10,11},{11... | collective-permute-start | bytes 196616 | tf_op jit(solution)/shard_map/while/body/eval_jaxpr/ppermute | solution.py:19
  149.6 7.3 %collective-permute-start.4 = (f32[1,1,32,256]{3,2,1,0:T(8,128)S(1)}, f32[1,1,32,256]{3,2,1,0:T(8,128)S(1)}, u32[]{:S(2)}, u32[]{:S(2)}) collective-permute-start(f32[1,1,32,256]{3,2,1,0:T(8,128)S(1)} %get-tuple-element.657), channel_id=1, source_target_pairs={{1,0},{2,1},{3,2},{4,3},{5,4},{6,5},{7,6},{9,8},{10,9},{11,10},{12... | collective-permute-start | bytes 98312 | tf_op jit(solution)/shard_map/while/body/eval_jaxpr/ppermute | solution.py:21
  150.9 7.6 %collective-permute-start.5 = (f32[1,1,32,256]{3,2,1,0:T(8,128)S(1)}, f32[1,1,32,256]{3,2,1,0:T(8,128)S(1)}, u32[]{:S(2)}, u32[]{:S(2)}) collective-permute-start(f32[1,1,32,256]{3,2,1,0:T(8,128)S(1)} %get-tuple-element.658), channel_id=1, source_target_pairs={{0,1},{1,2},{2,3},{3,4},{4,5},{5,6},{6,7},{8,9},{9,10},{10,11},{11... | collective-permute-start | bytes 98312 | tf_op jit(solution)/shard_map/while/body/eval_jaxpr/ppermute | solution.py:19
  160.6 11.8 %collective-permute-start.6 = (f32[2,1,1,32,256]{4,3,2,1,0:T(8,128)S(1)}, f32[2,1,1,32,256]{4,3,2,1,0:T(8,128)S(1)}, u32[]{:S(2)}, u32[]{:S(2)}) collective-permute-start(f32[2,1,1,32,256]{4,3,2,1,0:T(8,128)S(1)} %get-tuple-element.661), channel_id=1, source_target_pairs={{1,0},{2,1},{3,2},{4,3},{5,4},{6,5},{7,6},{9,8},{10,9},{11,10},{12... | collective-permute-start | bytes 196616 | tf_op jit(solution)/shard_map/while/body/eval_jaxpr/ppermute | solution.py:21
  162.1 10.4 %collective-permute-start.7 = (f32[2,1,1,32,256]{4,3,2,1,0:T(8,128)S(1)}, f32[2,1,1,32,256]{4,3,2,1,0:T(8,128)S(1)}, u32[]{:S(2)}, u32[]{:S(2)}) collective-permute-start(f32[2,1,1,32,256]{4,3,2,1,0:T(8,128)S(1)} %get-tuple-element.662), channel_id=1, source_target_pairs={{0,1},{1,2},{2,3},{3,4},{4,5},{5,6},{6,7},{8,9},{9,10},{10,11},{11... | collective-permute-start | bytes 196616 | tf_op jit(solution)/shard_map/while/body/eval_jaxpr/ppermute | solution.py:19
  173.6 7.4 %collective-permute-start = (f32[2,1,1,32,256]{4,3,2,1,0:T(8,128)S(1)}, f32[2,1,1,32,256]{4,3,2,1,0:T(8,128)S(1)}, u32[]{:S(2)}, u32[]{:S(2)}) collective-permute-start(f32[2,1,1,32,256]{4,3,2,1,0:T(8,128)S(1)} %get-tuple-element.643), channel_id=1, source_target_pairs={{1,0},{2,1},{3,2},{4,3},{5,4},{6,5},{7,6},{9,8},{10,9},{11,10},{12... | collective-permute-start | bytes 196616 | tf_op jit(solution)/shard_map/while/body/eval_jaxpr/ppermute | solution.py:21
  174.9 7.6 %collective-permute-start.1 = (f32[2,1,1,32,256]{4,3,2,1,0:T(8,128)S(1)}, f32[2,1,1,32,256]{4,3,2,1,0:T(8,128)S(1)}, u32[]{:S(2)}, u32[]{:S(2)}) collective-permute-start(f32[2,1,1,32,256]{4,3,2,1,0:T(8,128)S(1)} %get-tuple-element.644), channel_id=1, source_target_pairs={{0,1},{1,2},{2,3},{3,4},{4,5},{5,6},{6,7},{8,9},{9,10},{10,11},{11... | collective-permute-start | bytes 196616 | tf_op jit(solution)/shard_map/while/body/eval_jaxpr/ppermute | solution.py:19
  192.5 7.1 %collective-permute-start.4 = (f32[1,1,32,256]{3,2,1,0:T(8,128)S(1)}, f32[1,1,32,256]{3,2,1,0:T(8,128)S(1)}, u32[]{:S(2)}, u32[]{:S(2)}) collective-permute-start(f32[1,1,32,256]{3,2,1,0:T(8,128)S(1)} %get-tuple-element.657), channel_id=1, source_target_pairs={{1,0},{2,1},{3,2},{4,3},{5,4},{6,5},{7,6},{9,8},{10,9},{11,10},{12... | collective-permute-start | bytes 98312 | tf_op jit(solution)/shard_map/while/body/eval_jaxpr/ppermute | solution.py:21
  193.8 7.4 %collective-permute-start.5 = (f32[1,1,32,256]{3,2,1,0:T(8,128)S(1)}, f32[1,1,32,256]{3,2,1,0:T(8,128)S(1)}, u32[]{:S(2)}, u32[]{:S(2)}) collective-permute-start(f32[1,1,32,256]{3,2,1,0:T(8,128)S(1)} %get-tuple-element.658), channel_id=1, source_target_pairs={{0,1},{1,2},{2,3},{3,4},{4,5},{5,6},{6,7},{8,9},{9,10},{10,11},{11... | collective-permute-start | bytes 98312 | tf_op jit(solution)/shard_map/while/body/eval_jaxpr/ppermute | solution.py:19
  203.3 11.9 %collective-permute-start.6 = (f32[2,1,1,32,256]{4,3,2,1,0:T(8,128)S(1)}, f32[2,1,1,32,256]{4,3,2,1,0:T(8,128)S(1)}, u32[]{:S(2)}, u32[]{:S(2)}) collective-permute-start(f32[2,1,1,32,256]{4,3,2,1,0:T(8,128)S(1)} %get-tuple-element.661), channel_id=1, source_target_pairs={{1,0},{2,1},{3,2},{4,3},{5,4},{6,5},{7,6},{9,8},{10,9},{11,10},{12... | collective-permute-start | bytes 196616 | tf_op jit(solution)/shard_map/while/body/eval_jaxpr/ppermute | solution.py:21
  204.8 10.5 %collective-permute-start.7 = (f32[2,1,1,32,256]{4,3,2,1,0:T(8,128)S(1)}, f32[2,1,1,32,256]{4,3,2,1,0:T(8,128)S(1)}, u32[]{:S(2)}, u32[]{:S(2)}) collective-permute-start(f32[2,1,1,32,256]{4,3,2,1,0:T(8,128)S(1)} %get-tuple-element.662), channel_id=1, source_target_pairs={{0,1},{1,2},{2,3},{3,4},{4,5},{5,6},{6,7},{8,9},{9,10},{10,11},{11... | collective-permute-start | bytes 196616 | tf_op jit(solution)/shard_map/while/body/eval_jaxpr/ppermute | solution.py:19
  228.6 38.3 %all-to-all-start.2 = ((f32[4,1,4,32,256]{4,3,2,1,0:T(8,128)}), f32[4,1,4,32,256]{4,3,2,1,0:T(8,128)S(1)}, u32[]{:S(2)}, u32[]{:S(2)}) async-start(f32[4,1,4,32,256]{4,3,2,1,0:T(8,128)} %get-tuple-element.381), calls=%async_computation.2 | async-start | bytes 1048576 | tf_op jit(solution)/shard_map/all_to_all | solution.py:190
  (32 other events, 182.1 us)
